TPU v7x, 768 devices: a whole 4x8x12 slice. The times are simulated.
768 devices in a mesh: section: 8 (over y), fsdp: 96 (over z, x, core).
Axes of the slice: x: 4, y: 8, z: 12, core: 2. Of those that a mesh axis runs over, the one named last changes fastest.
Arguments:
- master: float32 [8, 768, 4096], P('section', 'fsdp'), may hold values from -0.12 to 0.12
- first_moment: float32 [8, 768, 4096], P('section', 'fsdp'), may hold values from -0.2 to 0.2
- second_moment: float32 [8, 768, 4096], P('section', 'fsdp'), may hold values from 0.25 to 1
- gradient: float32 [8, 768, 4096], P('section', 'fsdp'), may hold values from -64 to 64
Outputs:
- new_master: float32 [8, 768, 4096], P('section', 'fsdp')
- new_first: float32 [8, 768, 4096], P('section', 'fsdp')
- new_second: float32 [8, 768, 4096], P('section', 'fsdp')
- weights: bfloat16 [8, 768, 4096], P('section')
- grad_rms: float32 [], replicated
All inputs are finite; a program needn't handle non-finite values.
Results may differ from a plain program's by a relative error of at most 0.001.
Values may be sent and summed in bfloat16 or wider, within the bound.
No kernel may reach another device: no remote copies, remote signals or barrier semaphores. Data moves between devices by JAX's collectives and lax.ppermute only.
A program may use at most 64 MiB of HBM per device.

v0:
```python
import jax
import jax.numpy as jnp
from jax import lax
from jax.experimental import pallas as pl
from jax.experimental.pallas import tpu as pltpu
from jax.sharding import Mesh
from jax.sharding import PartitionSpec as P

FSDP = ("fsdp_0", "fsdp_1", "fsdp_2")
NZ, NX, NC = 12, 4, 2


BETA_ONE = 0.9
BETA_TWO = 0.95
LEARN_RATE = 0.05
DECAY = 0.1
EPSILON = 1e-08
BIAS_STEPS = 10.0


def taken_together(x, axis):
    count = lax.axis_size(axis)
    everything = lax.all_to_all(jnp.broadcast_to(x, (count, 1, 1)), axis, 0, 0, tiled=True)
    return jnp.sum(everything)


def adamw_part(master, first_moment, second_moment, gradient, clip_scale):
    scaled = clip_scale * gradient
    new_first = BETA_ONE * first_moment + (1.0 - BETA_ONE) * scaled
    new_second = BETA_TWO * second_moment + (1.0 - BETA_TWO) * scaled * scaled
    first_hat = new_first / (1.0 - BETA_ONE**BIAS_STEPS)
    second_hat = new_second / (1.0 - BETA_TWO**BIAS_STEPS)
    update = first_hat / (jnp.sqrt(second_hat) + EPSILON)
    new_master = master * (1.0 - LEARN_RATE * DECAY) - LEARN_RATE * update
    return (new_master, new_first, new_second)


def pairs(target):
    found = []
    for z in range(NZ):
        for x in range(NX):
            for c in range(NC):
                tz, tx, tc = target(z, x, c)
                found.append(((z * NX + x) * NC + c, ((tz % NZ) * NX + tx % NX) * NC + tc))
    return found


def far(step):
    return lambda z, x, c: (z + (step if z % 2 == 0 else -step), x, c)


def near(step, z_core):
    def target(z, x, c):
        if c != z_core:
            return z, x + (step if x % 2 == 0 else -step), c
        return z + (step if z % 2 == 0 else -step), x, c

    return target


def rows_of(place, piece, partner):
    z, x, c = place // (NX * NC), place // NC % NX, place % NC
    p, q = 1 - 2 * (z % 2), 1 - 2 * (x % 2)
    by_z = (z, z + p, z - p, z - 2 * p)
    by_x = (x, x + q, x - q, x + 2)
    core = 1 - c if partner else c
    rows = []
    for j in range(12):
        k2, k1 = j // 3, j % 3
        row_z = jnp.where(core == 0, by_z[piece], by_z[k2]) + NZ
        row_x = jnp.where(core == 0, by_x[k2], by_x[piece])
        row_z = row_z + (0, -4, 4)[k1] * (1 - 2 * (row_z % 2))
        rows.append(((row_z % NZ) * NX + (row_x + NX) % NX) * NC + core)
    return rows


def put(place, out, pieces):
    count = len(pieces)
    spec = pl.BlockSpec(memory_space=pl.ANY)

    def body(place, *refs):
        refs = refs[0 if out is None else 1 :]
        blocks, whole, sems = refs[:count], refs[count], refs[count + 1]
        copies = []
        for i, (_, piece, partner) in enumerate(pieces):
            for j, row in enumerate(rows_of(place[0], piece, partner)):
                copies.append(pltpu.make_async_copy(blocks[i].at[j], whole.at[row], sems.at[12 * i + j]))
        for copy in copies:
            copy.start()
        for copy in copies:
            copy.wait()

    first = pieces[0][0]
    return pl.pallas_call(
        body,
        out_shape=jax.ShapeDtypeStruct((NZ * NX * NC, *first.shape[1:]), first.dtype),
        in_specs=[pl.BlockSpec(memory_space=pltpu.SMEM)]
        + ([] if out is None else [spec])
        + [pl.BlockSpec(memory_space=pltpu.VMEM)] * count,
        out_specs=spec,
        scratch_shapes=[pltpu.SemaphoreType.DMA((12 * count,))],
        input_output_aliases={} if out is None else {1: 0},
        compiler_params=pltpu.CompilerParams(vmem_limit_bytes=4 * 2**20),
        name="put",
    )(place, *([] if out is None else [out]), *(p[0] for p in pieces))


def gathered(block):
    place = lax.axis_index(FSDP).astype(jnp.int32).reshape(1)
    sent = lambda x, target: lax.ppermute(x, FSDP, pairs(target))
    swap = lambda x: sent(x, lambda z, x, c: (z, x, 1 - c))
    one = jnp.concatenate([block, sent(block, far(4)), sent(block, far(-4))])
    parts = [one]
    for s in (1, -1, 2):
        parts.append(sent(one, near(s, 1)))
    two = jnp.concatenate(parts)
    own = [two]
    for s in (1, -1, 2):
        own.append(sent(two, near(s, 0)))
    other = {0: swap(own[0])}
    out = put(place, None, [(own[0], 0, False), (other[0], 0, True)])
    own[3], out = lax.optimization_barrier((own[3], out))
    other[3] = swap(own[3])
    out = put(place, out, [(own[3], 3, False)])
    own[1], out = lax.optimization_barrier((own[1], out))
    other[1] = swap(own[1])
    out = put(place, out, [(own[1], 1, False), (other[3], 3, True)])
    own[2], out = lax.optimization_barrier((own[2], out))
    other[2] = swap(own[2])
    out = put(place, out, [(own[2], 2, False), (other[1], 1, True)])
    out = put(place, out, [(other[2], 2, True)])
    return out.reshape(1, -1, block.shape[2])


def local(master, first_moment, second_moment, gradient):
    partial_sq = jnp.sum(gradient * gradient)
    squares = taken_together(taken_together(partial_sq, ("section", "fsdp_1", "fsdp_2")), "fsdp_0")
    grad_norm = jnp.sqrt(squares)
    param_count = float(
        lax.axis_size("section")
        * lax.axis_size(FSDP)
        * gradient.shape[0]
        * gradient.shape[1]
        * gradient.shape[2]
    )
    limit = jnp.float32(0.5 * param_count**0.5)
    clip_scale = limit / jnp.maximum(grad_norm, limit)
    grad_rms = grad_norm / jnp.float32(param_count**0.5)
    new_master, new_first, new_second = adamw_part(
        master, first_moment, second_moment, gradient, clip_scale
    )
    weights = gathered(new_master.astype(jnp.bfloat16))
    return (new_master, new_first, new_second, weights, grad_rms)


def solution(mesh):
    torus = Mesh(
        mesh.devices.reshape(mesh.shape["section"], NZ, NX, NC),
        ("section", *FSDP),
    )
    placed = (P("section", FSDP, None),) * 4
    return jax.shard_map(
        local,
        mesh=torus,
        in_specs=placed,
        out_specs=(
            P("section", FSDP, None),
            P("section", FSDP, None),
            P("section", FSDP, None),
            P("section", None, None),
            P(),
        ),
        check_vma=False,
    )
```

profile of v0, /device:TPU:1, one launch (start us, length us, event | category | flops | bytes accessed | tf_op | source)
XLA Modules:
  0.0 123.3 jit_solution(4425478645318710480)
XLA Ops:
  0.6 1.5 %multiply_reduce_fusion = f32[]{:T(128)} fusion(f32[1,8,4096]{2,1,0:T(8,128)} %param.7), kind=kLoop, calls=%fused_computation.5 | loop fusion | flops 65535 | bytes 131076 | tf_op jit(solution)/shard_map/reduce_sum | solution.py:136
  2.2 0.7 broadcast_in_dim.6
  2.8 23.2 %all_to_all.10 = f32[64,1,1]{2,1,0:T(1,128)S(1)} all-to-all(f32[64,1,1]{2,1,0:T(1,128)S(1)} %broadcast_in_dim.6), channel_id=1, replica_groups=mesh['section'=8,'fsdp_0'=12,'fsdp_1'=4,'fsdp_2'=2] {'section','fsdp_1',..., dimensions={0} | all-to-all | bytes 512 | tf_op jit(solution)/shard_map/all_to_all | solution.py:23
  26.1 0.7 reduce_sum.28
  26.7 0.6 broadcast_in_dim.7
  27.4 21.2 %all_to_all.11 = f32[12,1,1]{2,1,0:T(1,128)S(1)} all-to-all(f32[12,1,1]{2,1,0:T(1,128)S(1)} %broadcast_in_dim.7), channel_id=1, replica_groups=mesh['section'=8,'fsdp_0'=12,'fsdp_1'=4,'fsdp_2'=2] {'fsdp_0'}, dimensions={0} | all-to-all | bytes 96 | tf_op jit(solution)/shard_map/all_to_all | solution.py:23
  48.6 0.6 reduce_sum.29
  50.0 1.9 %constant_dynamic-update-slice_fusion.5 = (bf16[12,8,4096]{2,1,0:T(8,128)(2,1)S(1)}, bf16[1,8,4096]{2,1,0:T(8,128)(2,1)S(1)}, f32[1,8,4096]{2,1,0:T(8,128)}, f32[1,8,4096]{2,1,0:T(8,128)}, f32[1,8,4096]{2,1,0:T(8,128)}) fusion(f32[1,8,4096]{2,1,0:T(8,128)} %param.4, f32[1,8,4096]{2,1,0:T(8,128)} %param.7, f32[]{:T(128)S(6)} %div.21, f32[1,8,4096]{2,1,0:T(8,128)} %param.5, ...), kind=kLoop, calls=%fused_computation.11 | loop fusion | flops 524287 | bytes 1048580
  51.9 2.8 %collective-permute-start = (bf16[1,8,4096]{2,1,0:T(8,128)(2,1)S(1)}, bf16[1,8,4096]{2,1,0:T(8,128)(2,1)S(1)}, u32[]{:S(2)}, u32[]{:S(2)}) collective-permute-start(bf16[1,8,4096]{2,1,0:T(8,128)(2,1)S(1)} %get-tuple-element.18), channel_id=1, source_target_pairs={{0,32},{1,33},{2,34},{3,35},{4,36},{5,37},{6,38},{7,39},{8,72},{9,... | collective-permute-start | bytes 196616 | tf_op jit(solution)/shard_map/ppermute | solution.py:110
  54.6 6.4 %collective-permute-start.1 = (bf16[1,8,4096]{2,1,0:T(8,128)(2,1)S(1)}, bf16[1,8,4096]{2,1,0:T(8,128)(2,1)S(1)}, u32[]{:S(2)}, u32[]{:S(2)}) collective-permute-start(bf16[1,8,4096]{2,1,0:T(8,128)(2,1)S(1)} %get-tuple-element.18), channel_id=1, source_target_pairs={{0,64},{1,65},{2,66},{3,67},{4,68},{5,69},{6,70},{7,71},{8,40},{9,... | collective-permute-start | bytes 196616 | tf_op jit(solution)/shard_map/ppermute | solution.py:110
  61.1 4.0 %collective-permute-done.1 = bf16[1,8,4096]{2,1,0:T(8,128)(2,1)S(1)} collective-permute-done((bf16[1,8,4096]{2,1,0:T(8,128)(2,1)S(1)}, bf16[1,8,4096]{2,1,0:T(8,128)(2,1)S(1)}, u32[]{:S(2)}, u32[]{:S(2)}) %collective-permute-start.1) | collective-permute-done | bytes 65568 | tf_op jit(solution)/shard_map/ppermute | solution.py:110
  65.1 2.8 %collective-permute-start.2 = (bf16[3,8,4096]{2,1,0:T(8,128)(2,1)S(1)}, bf16[3,8,4096]{2,1,0:T(8,128)(2,1)S(1)}, u32[]{:S(2)}, u32[]{:S(2)}) collective-permute-start(bf16[3,8,4096]{2,1,0:T(8,128)(2,1)S(1)} %pad_maximum_fusion), channel_id=1, source_target_pairs={{0,2},{1,9},{2,0},{3,11},{4,6},{5,13},{6,4},{7,15},{8,10},{9,1},{1... | collective-permute-start | bytes 589832 | tf_op jit(solution)/shard_map/ppermute | solution.py:110
  67.9 2.5 %collective-permute-start.3 = (bf16[3,8,4096]{2,1,0:T(8,128)(2,1)S(1)}, bf16[3,8,4096]{2,1,0:T(8,128)(2,1)S(1)}, u32[]{:S(2)}, u32[]{:S(2)}) collective-permute-start(bf16[3,8,4096]{2,1,0:T(8,128)(2,1)S(1)} %pad_maximum_fusion), channel_id=1, source_target_pairs={{0,6},{1,89},{2,4},{3,91},{4,2},{5,93},{6,0},{7,95},{8,14},{9,17},... | collective-permute-start | bytes 589832 | tf_op jit(solution)/shard_map/ppermute | solution.py:110
  70.4 3.1 %collective-permute-start.4 = (bf16[3,8,4096]{2,1,0:T(8,128)(2,1)S(1)}, bf16[3,8,4096]{2,1,0:T(8,128)(2,1)S(1)}, u32[]{:S(2)}, u32[]{:S(2)}) collective-permute-start(bf16[3,8,4096]{2,1,0:T(8,128)(2,1)S(1)} %pad_maximum_fusion), channel_id=1, source_target_pairs={{0,4},{1,17},{2,6},{3,19},{4,0},{5,21},{6,2},{7,23},{8,12},{9,89},... | collective-permute-start | bytes 589832 | tf_op jit(solution)/shard_map/ppermute | solution.py:110
  73.6 0.0 collective-permute-done.2
  73.6 1.9 %collective-permute-done.3 = bf16[3,8,4096]{2,1,0:T(8,128)(2,1)S(1)} collective-permute-done((bf16[3,8,4096]{2,1,0:T(8,128)(2,1)S(1)}, bf16[3,8,4096]{2,1,0:T(8,128)(2,1)S(1)}, u32[]{:S(2)}, u32[]{:S(2)}) %collective-permute-start.3) | collective-permute-done | bytes 196640 | tf_op jit(solution)/shard_map/ppermute | solution.py:110
  75.6 3.4 %collective-permute-done.4 = bf16[3,8,4096]{2,1,0:T(8,128)(2,1)S(1)} collective-permute-done((bf16[3,8,4096]{2,1,0:T(8,128)(2,1)S(1)}, bf16[3,8,4096]{2,1,0:T(8,128)(2,1)S(1)}, u32[]{:S(2)}, u32[]{:S(2)}) %collective-permute-start.4) | collective-permute-done | bytes 196640 | tf_op jit(solution)/shard_map/ppermute | solution.py:110
  79.0 5.3 %collective-permute-start.8 = (bf16[12,8,4096]{2,1,0:T(8,128)(2,1)S(1)}, bf16[12,8,4096]{2,1,0:T(8,128)(2,1)S(1)}, u32[]{:S(2)}, u32[]{:S(2)}) collective-permute-start(bf16[12,8,4096]{2,1,0:T(8,128)(2,1)S(1)} %constant_dynamic-update-slice_fusion.refs_0_), channel_id=1, source_target_pairs={{0,1},{1,0},{2,3},{3,2},{4,5},{5,4},{6,7},{7,6},{8,9},{9,8},{10,11... | collective-permute-start | bytes 2359304 | tf_op jit(solution)/shard_map/ppermute | solution.py:110
  84.3 3.9 %collective-permute-start.7 = (bf16[12,8,4096]{2,1,0:T(8,128)(2,1)S(1)}, bf16[12,8,4096]{2,1,0:T(8,128)(2,1)}, u32[]{:S(2)}, u32[]{:S(2)}) collective-permute-start(bf16[12,8,4096]{2,1,0:T(8,128)(2,1)S(1)} %constant_dynamic-update-slice_fusion.refs_0_), channel_id=1, source_target_pairs={{0,16},{1,5},{2,18},{3,7},{4,20},{5,1},{6,22},{7,3},{8,88},{9,13},... | collective-permute-start | bytes 2359304 | tf_op jit(solution)/shard_map/ppermute | solution.py:110
  88.2 2.2 %collective-permute-start.6 = (bf16[12,8,4096]{2,1,0:T(8,128)(2,1)S(1)}, bf16[12,8,4096]{2,1,0:T(8,128)(2,1)S(1)}, u32[]{:S(2)}, u32[]{:S(2)}) collective-permute-start(bf16[12,8,4096]{2,1,0:T(8,128)(2,1)S(1)} %constant_dynamic-update-slice_fusion.refs_0_), channel_id=1, source_target_pairs={{0,8},{1,3},{2,10},{3,1},{4,12},{5,7},{6,14},{7,5},{8,0},{9,11},{1... | collective-permute-start | bytes 2359304 | tf_op jit(solution)/shard_map/ppermute | solution.py:110
  90.4 1.4 %put.5.refs_0_ = bf16[96,8,4096]{2,1,0:T(8,128)(2,1)} custom-call(s32[1]{0:T(128)} %bitcast.place, bf16[12,8,4096]{2,1,0:T(8,128)(2,1)S(1)} %constant_dynamic-update-slice_fusion.refs_0_, bf16[12,8,4096]{2,1,0:T(8,128)(2,1)S(1)} %collective-permute-done.8.refs_1_), custom_call_target="tpu_custom_call" | custom-call | tf_op jit(solution)/shard_map/put/pallas_call | solution.py:94
  91.8 7.1 %collective-permute-done.7.refs_1_ = bf16[12,8,4096]{2,1,0:T(8,128)(2,1)} collective-permute-done((bf16[12,8,4096]{2,1,0:T(8,128)(2,1)S(1)}, bf16[12,8,4096]{2,1,0:T(8,128)(2,1)}, u32[]{:S(2)}, u32[]{:S(2)}) %collective-permute-start.7) | collective-permute-done | bytes 786464 | tf_op jit(solution)/shard_map/ppermute | solution.py:110
  98.9 3.4 %collective-permute-start.9 = (bf16[12,8,4096]{2,1,0:T(8,128)(2,1)}, bf16[12,8,4096]{2,1,0:T(8,128)(2,1)S(1)}, u32[]{:S(2)}, u32[]{:S(2)}) collective-permute-start(bf16[12,8,4096]{2,1,0:T(8,128)(2,1)} %collective-permute-done.7.refs_1_), channel_id=1, source_target_pairs={{0,1},{1,0},{2,3},{3,2},{4,5},{5,4},{6,7},{7,6},{8,9},{9,8},{10,11... | collective-permute-start | bytes 2359304 | tf_op jit(solution)/shard_map/ppermute | solution.py:110
  102.3 3.6 %collective-permute-start.5 = (bf16[12,8,4096]{2,1,0:T(8,128)(2,1)S(1)}, bf16[12,8,4096]{2,1,0:T(8,128)(2,1)S(1)}, u32[]{:S(2)}, u32[]{:S(2)}) collective-permute-start(bf16[12,8,4096]{2,1,0:T(8,128)(2,1)S(1)} %constant_dynamic-update-slice_fusion.refs_0_), channel_id=1, source_target_pairs={{0,88},{1,7},{2,90},{3,5},{4,92},{5,3},{6,94},{7,1},{8,16},{9,15},... | collective-permute-start | bytes 2359304 | tf_op jit(solution)/shard_map/ppermute | solution.py:110
  105.9 2.1 %put.6.refs_0_ = bf16[96,8,4096]{2,1,0:T(8,128)(2,1)} custom-call(s32[1]{0:T(128)} %bitcast.place, bf16[96,8,4096]{2,1,0:T(8,128)(2,1)} %put.5.refs_0_, bf16[12,8,4096]{2,1,0:T(8,128)(2,1)} %collective-permute-done.7.refs_1_), custom_call_target="tpu_custom_call", output_to_operand_aliasing={{}: (1, {})} | custom-call | tf_op jit(solution)/shard_map/put/pallas_call | solution.py:94
  108.1 1.9 %collective-permute-start.10 = (bf16[12,8,4096]{2,1,0:T(8,128)(2,1)S(1)}, bf16[12,8,4096]{2,1,0:T(8,128)(2,1)S(1)}, u32[]{:S(2)}, u32[]{:S(2)}) collective-permute-start(bf16[12,8,4096]{2,1,0:T(8,128)(2,1)S(1)} %collective-permute-done.6.refs_1_), channel_id=1, source_target_pairs={{0,1},{1,0},{2,3},{3,2},{4,5},{5,4},{6,7},{7,6},{8,9},{9,8},{10,11... | collective-permute-start | bytes 2359304 | tf_op jit(solution)/shard_map/ppermute | solution.py:110
  110.0 1.4 %put.7.refs_0_ = bf16[96,8,4096]{2,1,0:T(8,128)(2,1)} custom-call(s32[1]{0:T(128)} %bitcast.place, bf16[96,8,4096]{2,1,0:T(8,128)(2,1)} %put.6.refs_0_, bf16[12,8,4096]{2,1,0:T(8,128)(2,1)S(1)} %collective-permute-done.6.refs_1_, bf16[12,8,4096]{2,1,0:T(8,128)(2,1)S(1)} %collective-permute-done.9.refs_2_), custom_call_target="tpu_custom_call", output_to_operand_aliasing={{}: (1, {})} | custom-call | tf_op jit(solution)/shard_map/put/pallas_call | solution.py:94
  111.4 5.2 %collective-permute-done.5.refs_1_ = bf16[12,8,4096]{2,1,0:T(8,128)(2,1)S(1)} collective-permute-done((bf16[12,8,4096]{2,1,0:T(8,128)(2,1)S(1)}, bf16[12,8,4096]{2,1,0:T(8,128)(2,1)S(1)}, u32[]{:S(2)}, u32[]{:S(2)}) %collective-permute-start.5) | collective-permute-done | bytes 786464 | tf_op jit(solution)/shard_map/ppermute | solution.py:110
  116.5 2.8 %collective-permute-start.11 = (bf16[12,8,4096]{2,1,0:T(8,128)(2,1)S(1)}, bf16[12,8,4096]{2,1,0:T(8,128)(2,1)S(1)}, u32[]{:S(2)}, u32[]{:S(2)}) collective-permute-start(bf16[12,8,4096]{2,1,0:T(8,128)(2,1)S(1)} %collective-permute-done.5.refs_1_), channel_id=1, source_target_pairs={{0,1},{1,0},{2,3},{3,2},{4,5},{5,4},{6,7},{7,6},{8,9},{9,8},{10,11... | collective-permute-start | bytes 2359304 | tf_op jit(solution)/shard_map/ppermute | solution.py:110
  119.3 1.4 %put.8.refs_0_ = bf16[96,8,4096]{2,1,0:T(8,128)(2,1)} custom-call(s32[1]{0:T(128)} %bitcast.place, bf16[96,8,4096]{2,1,0:T(8,128)(2,1)} %put.7.refs_0_, bf16[12,8,4096]{2,1,0:T(8,128)(2,1)S(1)} %collective-permute-done.5.refs_1_, bf16[12,8,4096]{2,1,0:T(8,128)(2,1)S(1)} %collective-permute-done.10.refs_2_), custom_call_target="tpu_custom_call", output_to_operand_aliasing={{}: (1, {})} | custom-call | tf_op jit(solution)/shard_map/put/pallas_call | solution.py:94
  120.7 0.5 collective-permute-done.11.refs_1_
  121.2 1.0 put.9
  (11 shorter events, 0.1 us)
Async XLA Ops:
  51.9 9.2 %collective-permute-start = (bf16[1,8,4096]{2,1,0:T(8,128)(2,1)S(1)}, bf16[1,8,4096]{2,1,0:T(8,128)(2,1)S(1)}, u32[]{:S(2)}, u32[]{:S(2)}) collective-permute-start(bf16[1,8,4096]{2,1,0:T(8,128)(2,1)S(1)} %get-tuple-element.18), channel_id=1, source_target_pairs={{0,32},{1,33},{2,34},{3,35},{4,36},{5,37},{6,38},{7,39},{8,72},{9,... | collective-permute-start | bytes 196616 | tf_op jit(solution)/shard_map/ppermute | solution.py:110
  54.6 10.5 %collective-permute-start.1 = (bf16[1,8,4096]{2,1,0:T(8,128)(2,1)S(1)}, bf16[1,8,4096]{2,1,0:T(8,128)(2,1)S(1)}, u32[]{:S(2)}, u32[]{:S(2)}) collective-permute-start(bf16[1,8,4096]{2,1,0:T(8,128)(2,1)S(1)} %get-tuple-element.18), channel_id=1, source_target_pairs={{0,64},{1,65},{2,66},{3,67},{4,68},{5,69},{6,70},{7,71},{8,40},{9,... | collective-permute-start | bytes 196616 | tf_op jit(solution)/shard_map/ppermute | solution.py:110
  65.1 8.4 %collective-permute-start.2 = (bf16[3,8,4096]{2,1,0:T(8,128)(2,1)S(1)}, bf16[3,8,4096]{2,1,0:T(8,128)(2,1)S(1)}, u32[]{:S(2)}, u32[]{:S(2)}) collective-permute-start(bf16[3,8,4096]{2,1,0:T(8,128)(2,1)S(1)} %pad_maximum_fusion), channel_id=1, source_target_pairs={{0,2},{1,9},{2,0},{3,11},{4,6},{5,13},{6,4},{7,15},{8,10},{9,1},{1... | collective-permute-start | bytes 589832 | tf_op jit(solution)/shard_map/ppermute | solution.py:110
  67.9 7.6 %collective-permute-start.3 = (bf16[3,8,4096]{2,1,0:T(8,128)(2,1)S(1)}, bf16[3,8,4096]{2,1,0:T(8,128)(2,1)S(1)}, u32[]{:S(2)}, u32[]{:S(2)}) collective-permute-start(bf16[3,8,4096]{2,1,0:T(8,128)(2,1)S(1)} %pad_maximum_fusion), channel_id=1, source_target_pairs={{0,6},{1,89},{2,4},{3,91},{4,2},{5,93},{6,0},{7,95},{8,14},{9,17},... | collective-permute-start | bytes 589832 | tf_op jit(solution)/shard_map/ppermute | solution.py:110
  70.4 8.5 %collective-permute-start.4 = (bf16[3,8,4096]{2,1,0:T(8,128)(2,1)S(1)}, bf16[3,8,4096]{2,1,0:T(8,128)(2,1)S(1)}, u32[]{:S(2)}, u32[]{:S(2)}) collective-permute-start(bf16[3,8,4096]{2,1,0:T(8,128)(2,1)S(1)} %pad_maximum_fusion), channel_id=1, source_target_pairs={{0,4},{1,17},{2,6},{3,19},{4,0},{5,21},{6,2},{7,23},{8,12},{9,89},... | collective-permute-start | bytes 589832 | tf_op jit(solution)/shard_map/ppermute | solution.py:110
  79.0 11.5 %collective-permute-start.8 = (bf16[12,8,4096]{2,1,0:T(8,128)(2,1)S(1)}, bf16[12,8,4096]{2,1,0:T(8,128)(2,1)S(1)}, u32[]{:S(2)}, u32[]{:S(2)}) collective-permute-start(bf16[12,8,4096]{2,1,0:T(8,128)(2,1)S(1)} %constant_dynamic-update-slice_fusion.refs_0_), channel_id=1, source_target_pairs={{0,1},{1,0},{2,3},{3,2},{4,5},{5,4},{6,7},{7,6},{8,9},{9,8},{10,11... | collective-permute-start | bytes 2359304 | tf_op jit(solution)/shard_map/ppermute | solution.py:110
  84.3 14.6 %collective-permute-start.7 = (bf16[12,8,4096]{2,1,0:T(8,128)(2,1)S(1)}, bf16[12,8,4096]{2,1,0:T(8,128)(2,1)}, u32[]{:S(2)}, u32[]{:S(2)}) collective-permute-start(bf16[12,8,4096]{2,1,0:T(8,128)(2,1)S(1)} %constant_dynamic-update-slice_fusion.refs_0_), channel_id=1, source_target_pairs={{0,16},{1,5},{2,18},{3,7},{4,20},{5,1},{6,22},{7,3},{8,88},{9,13},... | collective-permute-start | bytes 2359304 | tf_op jit(solution)/shard_map/ppermute | solution.py:110
  88.2 19.9 %collective-permute-start.6 = (bf16[12,8,4096]{2,1,0:T(8,128)(2,1)S(1)}, bf16[12,8,4096]{2,1,0:T(8,128)(2,1)S(1)}, u32[]{:S(2)}, u32[]{:S(2)}) collective-permute-start(bf16[12,8,4096]{2,1,0:T(8,128)(2,1)S(1)} %constant_dynamic-update-slice_fusion.refs_0_), channel_id=1, source_target_pairs={{0,8},{1,3},{2,10},{3,1},{4,12},{5,7},{6,14},{7,5},{8,0},{9,11},{1... | collective-permute-start | bytes 2359304 | tf_op jit(solution)/shard_map/ppermute | solution.py:110
  98.9 11.1 %collective-permute-start.9 = (bf16[12,8,4096]{2,1,0:T(8,128)(2,1)}, bf16[12,8,4096]{2,1,0:T(8,128)(2,1)S(1)}, u32[]{:S(2)}, u32[]{:S(2)}) collective-permute-start(bf16[12,8,4096]{2,1,0:T(8,128)(2,1)} %collective-permute-done.7.refs_1_), channel_id=1, source_target_pairs={{0,1},{1,0},{2,3},{3,2},{4,5},{5,4},{6,7},{7,6},{8,9},{9,8},{10,11... | collective-permute-start | bytes 2359304 | tf_op jit(solution)/shard_map/ppermute | solution.py:110
  102.3 14.2 %collective-permute-start.5 = (bf16[12,8,4096]{2,1,0:T(8,128)(2,1)S(1)}, bf16[12,8,4096]{2,1,0:T(8,128)(2,1)S(1)}, u32[]{:S(2)}, u32[]{:S(2)}) collective-permute-start(bf16[12,8,4096]{2,1,0:T(8,128)(2,1)S(1)} %constant_dynamic-update-slice_fusion.refs_0_), channel_id=1, source_target_pairs={{0,88},{1,7},{2,90},{3,5},{4,92},{5,3},{6,94},{7,1},{8,16},{9,15},... | collective-permute-start | bytes 2359304 | tf_op jit(solution)/shard_map/ppermute | solution.py:110
  108.1 11.2 %collective-permute-start.10 = (bf16[12,8,4096]{2,1,0:T(8,128)(2,1)S(1)}, bf16[12,8,4096]{2,1,0:T(8,128)(2,1)S(1)}, u32[]{:S(2)}, u32[]{:S(2)}) collective-permute-start(bf16[12,8,4096]{2,1,0:T(8,128)(2,1)S(1)} %collective-permute-done.6.refs_1_), channel_id=1, source_target_pairs={{0,1},{1,0},{2,3},{3,2},{4,5},{5,4},{6,7},{7,6},{8,9},{9,8},{10,11... | collective-permute-start | bytes 2359304 | tf_op jit(solution)/shard_map/ppermute | solution.py:110
  116.5 4.7 %collective-permute-start.11 = (bf16[12,8,4096]{2,1,0:T(8,128)(2,1)S(1)}, bf16[12,8,4096]{2,1,0:T(8,128)(2,1)S(1)}, u32[]{:S(2)}, u32[]{:S(2)}) collective-permute-start(bf16[12,8,4096]{2,1,0:T(8,128)(2,1)S(1)} %collective-permute-done.5.refs_1_), channel_id=1, source_target_pairs={{0,1},{1,0},{2,3},{3,2},{4,5},{5,4},{6,7},{7,6},{8,9},{9,8},{10,11... | collective-permute-start | bytes 2359304 | tf_op jit(solution)/shard_map/ppermute | solution.py:110
where the time goes:
time: 124 us; the launch traced here: 123 us
  blocking collectives  44.4 us (36%)
  starting transfers between devices  40.7 us (33%)
  waiting for transfers between devices  22.2 us (18%)
  Pallas kernels  7.15 us (6%)
  other arithmetic  4.74 us (4%)
  between operations  2.74 us (2%)
  local copies, waits for them, and re-layouts  1.37 us (1%)
    all_to_all x2, blocking collectives, taken_together(): lax.all_to_all(jnp.broadcast_to(x, (count, 1, 1)), axis, 0, 0, tiled=True)  44.4 us
    ppermute x12, starting transfers between devices, gathered(): sent = lambda x, target: lax.ppermute(x, FSDP, pairs(target))  40.7 us
    ppermute x12, waiting for transfers between devices, gathered(): sent = lambda x, target: lax.ppermute(x, FSDP, pairs(target))  22.2 us
    pallas_call x5, Pallas kernels, put(): pl.pallas_call(body, out_shape=jax.ShapeDtypeStruct((NZ * NX * NC, *first...  7.15 us
  transfers between devices with their start and end apart: 12, of which 6 were waited for; matrix products, arithmetic and copies ran while one was open for 0% of the time, Pallas kernels for 5%

commit v1 on v0

--- a/solution.py
+++ b/solution.py
@@ -8,6 +8,7 @@
 
 FSDP = ("fsdp_0", "fsdp_1", "fsdp_2")
 NZ, NX, NC = 12, 4, 2
+ROWS_DEV = 8
 
 
 BETA_ONE = 0.9
@@ -18,10 +19,55 @@
 BIAS_STEPS = 10.0
 
 
-def taken_together(x, axis):
-    count = lax.axis_size(axis)
-    everything = lax.all_to_all(jnp.broadcast_to(x, (count, 1, 1)), axis, 0, 0, tiled=True)
-    return jnp.sum(everything)
+def small(**limits):
+    return pltpu.CompilerParams(vmem_limit_bytes=limits.get("mib", 4) * 2**20)
+
+
+def swapped(x, axis):
+    return lax.all_to_all(x, axis, 0, 0, tiled=True)
+
+
+def spread_squares(count, *state):
+    def body(*refs):
+        arrays, out, held, sems = refs[:4], refs[4], refs[5:9], refs[9]
+        copies = [pltpu.make_async_copy(a, h, sems.at[i]) for i, (a, h) in enumerate(zip(arrays, held))]
+        for copy in reversed(copies):
+            copy.start()
+        copies[-1].wait()
+        gradient = held[-1][0]
+        lanes = (gradient * gradient).reshape(ROWS_DEV, -1, 128).sum(axis=(0, 1))
+        out[...] = jnp.broadcast_to(lanes[None, None], out.shape)
+        for copy in copies[:-1]:
+            copy.wait()
+
+    return pl.pallas_call(
+        body,
+        out_shape=[jax.ShapeDtypeStruct((count, 1, 128), jnp.float32)]
+        + [jax.ShapeDtypeStruct(a.shape, a.dtype) for a in state],
+        in_specs=[pl.BlockSpec(memory_space=pltpu.HBM)] * 4,
+        out_specs=[pl.BlockSpec(memory_space=pltpu.VMEM)] * 5,
+        scratch_shapes=[pltpu.SemaphoreType.DMA((4,))],
+        compiler_params=small(),
+        name="spread_squares",
+    )(*state)
+
+
+def summed_and_spread(sums, count):
+    def body(s, out):
+        out[...] = jnp.broadcast_to(jnp.sum(s[...], axis=0, keepdims=True), out.shape)
+
+    return pl.pallas_call(
+        body,
+        out_shape=jax.ShapeDtypeStruct((count, 1, 128), jnp.float32),
+        in_specs=[pl.BlockSpec(memory_space=pltpu.VMEM)],
+        out_specs=pl.BlockSpec(memory_space=pltpu.VMEM),
+        compiler_params=small(),
+        name="summed_and_spread",
+    )(sums)
+
+
+def norm_of(sums):
+    return jnp.sqrt(jnp.sum(sums, axis=(0, 1, 2), keepdims=True)[0])
 
 
 def adamw_part(master, first_moment, second_moment, gradient, clip_scale):
@@ -33,6 +79,32 @@
     update = first_hat / (jnp.sqrt(second_hat) + EPSILON)
     new_master = master * (1.0 - LEARN_RATE * DECAY) - LEARN_RATE * update
     return (new_master, new_first, new_second)
+
+
+def stepped(sums, param_count, master, first_moment, second_moment, gradient, weights_only):
+    limit = 0.5 * param_count**0.5
+
+    def body(s, p, m, v, g, *outs):
+        norm = norm_of(s[...])
+        scale = limit / jnp.maximum(norm, limit)
+        new = adamw_part(p[0], m[0], v[0], g[0], scale)
+        if weights_only:
+            outs[0][0] = new[0].astype(jnp.bfloat16)
+            return
+        for out, value in zip(outs, new):
+            out[0] = value
+        outs[3][...] = jnp.broadcast_to(norm / param_count**0.5, (1, 128))
+
+    like = lambda dtype: jax.ShapeDtypeStruct(master.shape, dtype)
+    out_shape = [like(jnp.bfloat16)] if weights_only else [like(jnp.float32)] * 3 + [jax.ShapeDtypeStruct((1, 128), jnp.float32)]
+    return pl.pallas_call(
+        body,
+        out_shape=out_shape,
+        in_specs=[pl.BlockSpec(memory_space=pltpu.VMEM)] * 5,
+        out_specs=[pl.BlockSpec(memory_space=pltpu.VMEM)] * len(out_shape),
+        compiler_params=small(),
+        name="weights" if weights_only else "state",
+    )(sums, master, first_moment, second_moment, gradient)
 
 
 def pairs(target):
@@ -105,11 +177,12 @@
     )(place, *([] if out is None else [out]), *(p[0] for p in pieces))
 
 
-def gathered(block):
+def gathered(block, meanwhile):
     place = lax.axis_index(FSDP).astype(jnp.int32).reshape(1)
     sent = lambda x, target: lax.ppermute(x, FSDP, pairs(target))
     swap = lambda x: sent(x, lambda z, x, c: (z, x, 1 - c))
-    one = jnp.concatenate([block, sent(block, far(4)), sent(block, far(-4))])
+    above, below, beside = lax.optimization_barrier((sent(block, far(4)), sent(block, far(-4)), meanwhile()))
+    one = jnp.concatenate([block, above, below])
     parts = [one]
     for s in (1, -1, 2):
         parts.append(sent(one, near(s, 1)))
@@ -124,18 +197,13 @@
     out = put(place, out, [(own[3], 3, False)])
     own[1], out = lax.optimization_barrier((own[1], out))
     other[1] = swap(own[1])
-    out = put(place, out, [(own[1], 1, False), (other[3], 3, True)])
-    own[2], out = lax.optimization_barrier((own[2], out))
     other[2] = swap(own[2])
-    out = put(place, out, [(own[2], 2, False), (other[1], 1, True)])
-    out = put(place, out, [(other[2], 2, True)])
-    return out.reshape(1, -1, block.shape[2])
+    out = put(place, out, [(own[1], 1, False), (own[2], 2, False), (other[3], 3, True)])
+    out = put(place, out, [(other[1], 1, True), (other[2], 2, True)])
+    return out.reshape(1, -1, block.shape[2]), beside
 
 
 def local(master, first_moment, second_moment, gradient):
-    partial_sq = jnp.sum(gradient * gradient)
-    squares = taken_together(taken_together(partial_sq, ("section", "fsdp_1", "fsdp_2")), "fsdp_0")
-    grad_norm = jnp.sqrt(squares)
     param_count = float(
         lax.axis_size("section")
         * lax.axis_size(FSDP)
@@ -143,14 +211,14 @@
         * gradient.shape[1]
         * gradient.shape[2]
     )
-    limit = jnp.float32(0.5 * param_count**0.5)
-    clip_scale = limit / jnp.maximum(grad_norm, limit)
-    grad_rms = grad_norm / jnp.float32(param_count**0.5)
-    new_master, new_first, new_second = adamw_part(
-        master, first_moment, second_moment, gradient, clip_scale
-    )
-    weights = gathered(new_master.astype(jnp.bfloat16))
-    return (new_master, new_first, new_second, weights, grad_rms)
+    plane = ("section", "fsdp_1", "fsdp_2")
+    sums, *state = spread_squares(lax.axis_size(plane), master, first_moment, second_moment, gradient)
+    sums = swapped(summed_and_spread(swapped(sums, plane), NZ), "fsdp_0")
+    (block,) = stepped(sums, param_count, *state, True)
+    weights, (new_master, new_first, new_second, rms) = gathered(
+        block, lambda: stepped(sums, param_count, *state, False)
+    )
+    return (new_master, new_first, new_second, weights, rms[0, 0])
 
 
 def solution(mesh):

time: 124 us -> 113 us (0.911)
  waiting for transfers between devices: 22.2 us -> 15 us
  other arithmetic: 4.74 us -> 0.02 us
  local copies, waits for them, and re-layouts: 1.37 us -> 3.67 us
  between operations: 2.74 us -> 0.88 us
  Pallas kernels: 7.15 us -> 8.58 us
    ppermute x12, waiting for transfers between devices: 22.2 us -> 15 us  [gathered(): sent = lambda x, target: lax.ppermute(x, FSDP, pairs(target))]
    unnamed x4 -> x13, local copies, waits for them, and re-layouts: 0.04 us -> 3.66 us
    reduce_sum x3 -> x0, other arithmetic: 2.82 us -> none  [the longest x1 1.54 us: local(): partial_sq = jnp.sum(gradient * gradient)]
    pallas_call x0 -> x4, Pallas kernels: none -> 2.07 us  [the longest x2 1.25 us: stepped(): pl.pallas_call(body, out_shape=out_shape, in_specs=[pl.BlockSpec(memory_s...]
    unnamed x1 -> x0, other arithmetic: 1.9 us -> none
    broadcast_in_dim x2 -> x0, local copies, waits for them, and re-layouts: 1.31 us -> none  [taken_together(): jnp.broadcast_to(x, (count, 1, 1))]
    pallas_call x5 -> x4, Pallas kernels: 7.15 us -> 6.51 us  [put(): pl.pallas_call(body, out_shape=jax.ShapeDtypeStruct((NZ * NX * NC, *first...]
where the time goes in v1:
time: 113 us; the launch traced here: 112 us
  blocking collectives  44.4 us (39%)
  starting transfers between devices  39.6 us (35%)
  waiting for transfers between devices  15 us (13%)
  Pallas kernels  8.58 us (8%)
  local copies, waits for them, and re-layouts  3.67 us (3%)
    all_to_all x2, blocking collectives, swapped(): return lax.all_to_all(x, axis, 0, 0, tiled=True)  44.4 us
    ppermute x12, starting transfers between devices, gathered(): sent = lambda x, target: lax.ppermute(x, FSDP, pairs(target))  39.6 us
    ppermute x12, waiting for transfers between devices, gathered(): sent = lambda x, target: lax.ppermute(x, FSDP, pairs(target))  15 us
    pallas_call x4, Pallas kernels, put(): pl.pallas_call(body, out_shape=jax.ShapeDtypeStruct((NZ * NX * NC, *first...  6.51 us
    unnamed x13, local copies, waits for them, and re-layouts  3.66 us
  transfers between devices with their start and end apart: 12, of which 6 were waited for; matrix products, arithmetic and copies ran while one was open for 0% of the time, Pallas kernels for 5%

profile of v1, /device:TPU:1, one launch (start us, length us, event | category | flops | bytes accessed | tf_op | source)
XLA Modules:
  0.0 112.1 jit_solution(2757021660053876004)
XLA Ops:
  0.6 0.9 copy-done
  1.5 0.9 copy-done.1
  2.4 0.9 copy-done.2
  3.3 0.9 copy-done.3
  4.3 0.8 spread_squares.1
  5.0 23.2 %all_to_all.10.s = f32[64,1,128]{2,1,0:T(1,128)S(1)} all-to-all(f32[64,1,128]{2,1,0:T(1,128)S(1)} %get-tuple-element.24), channel_id=1, replica_groups=mesh['section'=8,'fsdp_0'=12,'fsdp_1'=4,'fsdp_2'=2] {'section','fsdp_1',..., dimensions={0} | all-to-all | bytes 65536 | tf_op jit(solution)/shard_map/all_to_all | solution.py:27
  28.2 0.1 summed_and_spread.1
  28.3 21.2 %all_to_all.11.s = f32[12,1,128]{2,1,0:T(1,128)S(1)} all-to-all(f32[12,1,128]{2,1,0:T(1,128)S(1)} %summed_and_spread.1), channel_id=1, replica_groups=mesh['section'=8,'fsdp_0'=12,'fsdp_1'=4,'fsdp_2'=2] {'fsdp_0'}, dimensions={0} | all-to-all | bytes 12288 | tf_op jit(solution)/shard_map/all_to_all | solution.py:27
  49.5 0.3 weights.1
  49.8 2.8 %collective-permute-start = (bf16[1,8,4096]{2,1,0:T(8,128)(2,1)S(1)}, bf16[1,8,4096]{2,1,0:T(8,128)(2,1)S(1)}, u32[]{:S(2)}, u32[]{:S(2)}) collective-permute-start(bf16[1,8,4096]{2,1,0:T(8,128)(2,1)S(1)} %weights.1), channel_id=1, source_target_pairs={{0,32},{1,33},{2,34},{3,35},{4,36},{5,37},{6,38},{7,39},{8,72},{9,... | collective-permute-start | bytes 196616 | tf_op jit(solution)/shard_map/ppermute | solution.py:182
  52.6 6.4 %collective-permute-start.1 = (bf16[1,8,4096]{2,1,0:T(8,128)(2,1)S(1)}, bf16[1,8,4096]{2,1,0:T(8,128)(2,1)S(1)}, u32[]{:S(2)}, u32[]{:S(2)}) collective-permute-start(bf16[1,8,4096]{2,1,0:T(8,128)(2,1)S(1)} %weights.1), channel_id=1, source_target_pairs={{0,64},{1,65},{2,66},{3,67},{4,68},{5,69},{6,70},{7,71},{8,40},{9,... | collective-permute-start | bytes 196616 | tf_op jit(solution)/shard_map/ppermute | solution.py:182
  59.0 1.0 state.1
  60.0 3.1 %collective-permute-done.1 = bf16[1,8,4096]{2,1,0:T(8,128)(2,1)S(1)} collective-permute-done((bf16[1,8,4096]{2,1,0:T(8,128)(2,1)S(1)}, bf16[1,8,4096]{2,1,0:T(8,128)(2,1)S(1)}, u32[]{:S(2)}, u32[]{:S(2)}) %collective-permute-start.1) | collective-permute-done | bytes 65568 | tf_op jit(solution)/shard_map/ppermute | solution.py:182
  63.1 2.8 %collective-permute-start.2 = (bf16[3,8,4096]{2,1,0:T(8,128)(2,1)S(1)}, bf16[3,8,4096]{2,1,0:T(8,128)(2,1)S(1)}, u32[]{:S(2)}, u32[]{:S(2)}) collective-permute-start(bf16[3,8,4096]{2,1,0:T(8,128)(2,1)S(1)} %pad_maximum_fusion), channel_id=1, source_target_pairs={{0,2},{1,9},{2,0},{3,11},{4,6},{5,13},{6,4},{7,15},{8,10},{9,1},{1... | collective-permute-start | bytes 589832 | tf_op jit(solution)/shard_map/ppermute | solution.py:182
  65.9 2.5 %collective-permute-start.3 = (bf16[3,8,4096]{2,1,0:T(8,128)(2,1)S(1)}, bf16[3,8,4096]{2,1,0:T(8,128)(2,1)S(1)}, u32[]{:S(2)}, u32[]{:S(2)}) collective-permute-start(bf16[3,8,4096]{2,1,0:T(8,128)(2,1)S(1)} %pad_maximum_fusion), channel_id=1, source_target_pairs={{0,6},{1,89},{2,4},{3,91},{4,2},{5,93},{6,0},{7,95},{8,14},{9,17},... | collective-permute-start | bytes 589832 | tf_op jit(solution)/shard_map/ppermute | solution.py:182
  68.4 3.1 %collective-permute-start.4 = (bf16[3,8,4096]{2,1,0:T(8,128)(2,1)S(1)}, bf16[3,8,4096]{2,1,0:T(8,128)(2,1)S(1)}, u32[]{:S(2)}, u32[]{:S(2)}) collective-permute-start(bf16[3,8,4096]{2,1,0:T(8,128)(2,1)S(1)} %pad_maximum_fusion), channel_id=1, source_target_pairs={{0,4},{1,17},{2,6},{3,19},{4,0},{5,21},{6,2},{7,23},{8,12},{9,89},... | collective-permute-start | bytes 589832 | tf_op jit(solution)/shard_map/ppermute | solution.py:182
  71.6 1.9 %collective-permute-done.3 = bf16[3,8,4096]{2,1,0:T(8,128)(2,1)S(1)} collective-permute-done((bf16[3,8,4096]{2,1,0:T(8,128)(2,1)S(1)}, bf16[3,8,4096]{2,1,0:T(8,128)(2,1)S(1)}, u32[]{:S(2)}, u32[]{:S(2)}) %collective-permute-start.3) | collective-permute-done | bytes 196640 | tf_op jit(solution)/shard_map/ppermute | solution.py:182
  73.5 3.4 %collective-permute-done.4 = bf16[3,8,4096]{2,1,0:T(8,128)(2,1)S(1)} collective-permute-done((bf16[3,8,4096]{2,1,0:T(8,128)(2,1)S(1)}, bf16[3,8,4096]{2,1,0:T(8,128)(2,1)S(1)}, u32[]{:S(2)}, u32[]{:S(2)}) %collective-permute-start.4) | collective-permute-done | bytes 196640 | tf_op jit(solution)/shard_map/ppermute | solution.py:182
  76.9 5.3 %collective-permute-start.7 = (bf16[12,8,4096]{2,1,0:T(8,128)(2,1)S(1)}, bf16[12,8,4096]{2,1,0:T(8,128)(2,1)}, u32[]{:S(2)}, u32[]{:S(2)}) collective-permute-start(bf16[12,8,4096]{2,1,0:T(8,128)(2,1)S(1)} %constant_dynamic-update-slice_fusion.refs_0_), channel_id=1, source_target_pairs={{0,1},{1,0},{2,3},{3,2},{4,5},{5,4},{6,7},{7,6},{8,9},{9,8},{10,11... | collective-permute-start | bytes 2359304 | tf_op jit(solution)/shard_map/ppermute | solution.py:182
  82.2 3.9 %collective-permute-start.6 = (bf16[12,8,4096]{2,1,0:T(8,128)(2,1)S(1)}, bf16[12,8,4096]{2,1,0:T(8,128)(2,1)S(1)}, u32[]{:S(2)}, u32[]{:S(2)}) collective-permute-start(bf16[12,8,4096]{2,1,0:T(8,128)(2,1)S(1)} %constant_dynamic-update-slice_fusion.refs_0_), channel_id=1, source_target_pairs={{0,16},{1,5},{2,18},{3,7},{4,20},{5,1},{6,22},{7,3},{8,88},{9,13},... | collective-permute-start | bytes 2359304 | tf_op jit(solution)/shard_map/ppermute | solution.py:182
  86.2 2.2 %collective-permute-start.5 = (bf16[12,8,4096]{2,1,0:T(8,128)(2,1)S(1)}, bf16[12,8,4096]{2,1,0:T(8,128)(2,1)S(1)}, u32[]{:S(2)}, u32[]{:S(2)}) collective-permute-start(bf16[12,8,4096]{2,1,0:T(8,128)(2,1)S(1)} %constant_dynamic-update-slice_fusion.refs_0_), channel_id=1, source_target_pairs={{0,8},{1,3},{2,10},{3,1},{4,12},{5,7},{6,14},{7,5},{8,0},{9,11},{1... | collective-permute-start | bytes 2359304 | tf_op jit(solution)/shard_map/ppermute | solution.py:182
  88.4 2.9 %collective-permute-start.8 = (bf16[12,8,4096]{2,1,0:T(8,128)(2,1)S(1)}, bf16[12,8,4096]{2,1,0:T(8,128)(2,1)S(1)}, u32[]{:S(2)}, u32[]{:S(2)}) collective-permute-start(bf16[12,8,4096]{2,1,0:T(8,128)(2,1)S(1)} %constant_dynamic-update-slice_fusion.refs_0_), channel_id=1, source_target_pairs={{0,88},{1,7},{2,90},{3,5},{4,92},{5,3},{6,94},{7,1},{8,16},{9,15},... | collective-permute-start | bytes 2359304 | tf_op jit(solution)/shard_map/ppermute | solution.py:182
  91.3 2.5 %put.4.refs_0_ = bf16[96,8,4096]{2,1,0:T(8,128)(2,1)} custom-call(s32[1]{0:T(128)} %bitcast.place, bf16[12,8,4096]{2,1,0:T(8,128)(2,1)S(1)} %constant_dynamic-update-slice_fusion.refs_0_, bf16[12,8,4096]{2,1,0:T(8,128)(2,1)} %collective-permute-done.7.refs_1_), custom_call_target="tpu_custom_call" | custom-call | tf_op jit(solution)/shard_map/put/pallas_call | solution.py:166
  93.7 3.1 %collective-permute-done.6.refs_1_ = bf16[12,8,4096]{2,1,0:T(8,128)(2,1)S(1)} collective-permute-done((bf16[12,8,4096]{2,1,0:T(8,128)(2,1)S(1)}, bf16[12,8,4096]{2,1,0:T(8,128)(2,1)S(1)}, u32[]{:S(2)}, u32[]{:S(2)}) %collective-permute-start.6) | collective-permute-done | bytes 786464 | tf_op jit(solution)/shard_map/ppermute | solution.py:182
  96.8 3.4 %collective-permute-start.9 = (bf16[12,8,4096]{2,1,0:T(8,128)(2,1)S(1)}, bf16[12,8,4096]{2,1,0:T(8,128)(2,1)S(1)}, u32[]{:S(2)}, u32[]{:S(2)}) collective-permute-start(bf16[12,8,4096]{2,1,0:T(8,128)(2,1)S(1)} %collective-permute-done.6.refs_1_), channel_id=1, source_target_pairs={{0,1},{1,0},{2,3},{3,2},{4,5},{5,4},{6,7},{7,6},{8,9},{9,8},{10,11... | collective-permute-start | bytes 2359304 | tf_op jit(solution)/shard_map/ppermute | solution.py:182
  100.3 1.0 put.5.refs_0_
  101.3 3.3 %collective-permute-done.5.refs_1_ = bf16[12,8,4096]{2,1,0:T(8,128)(2,1)S(1)} collective-permute-done((bf16[12,8,4096]{2,1,0:T(8,128)(2,1)S(1)}, bf16[12,8,4096]{2,1,0:T(8,128)(2,1)S(1)}, u32[]{:S(2)}, u32[]{:S(2)}) %collective-permute-start.5) | collective-permute-done | bytes 786464 | tf_op jit(solution)/shard_map/ppermute | solution.py:182
  104.6 1.9 %collective-permute-start.10 = (bf16[12,8,4096]{2,1,0:T(8,128)(2,1)S(1)}, bf16[12,8,4096]{2,1,0:T(8,128)(2,1)S(1)}, u32[]{:S(2)}, u32[]{:S(2)}) collective-permute-start(bf16[12,8,4096]{2,1,0:T(8,128)(2,1)S(1)} %collective-permute-done.5.refs_1_), channel_id=1, source_target_pairs={{0,1},{1,0},{2,3},{3,2},{4,5},{5,4},{6,7},{7,6},{8,9},{9,8},{10,11... | collective-permute-start | bytes 2359304 | tf_op jit(solution)/shard_map/ppermute | solution.py:182
  106.5 2.4 %collective-permute-start.11 = (bf16[12,8,4096]{2,1,0:T(8,128)(2,1)S(1)}, bf16[12,8,4096]{2,1,0:T(8,128)(2,1)S(1)}, u32[]{:S(2)}, u32[]{:S(2)}) collective-permute-start(bf16[12,8,4096]{2,1,0:T(8,128)(2,1)S(1)} %collective-permute-done.8.refs_2_), channel_id=1, source_target_pairs={{0,1},{1,0},{2,3},{3,2},{4,5},{5,4},{6,7},{7,6},{8,9},{9,8},{10,11... | collective-permute-start | bytes 2359304 | tf_op jit(solution)/shard_map/ppermute | solution.py:182
  108.9 1.7 %put.6.refs_0_ = bf16[96,8,4096]{2,1,0:T(8,128)(2,1)} custom-call(s32[1]{0:T(128)} %bitcast.place, bf16[96,8,4096]{2,1,0:T(8,128)(2,1)} %put.5.refs_0_, bf16[12,8,4096]{2,1,0:T(8,128)(2,1)S(1)} %collective-permute-done.5.refs_1_, bf16[12,8,4096]{2,1,0:T(8,128)(2,1)S(1)} %collective-permute-done.8.refs_2_, ...), custom_call_target="tpu_custom_call", output_to_operand_aliasing={{}: (1, {})} | custom-call | tf_op jit(solution)/shard_map/put/pallas_call | solution.py:166
  110.7 0.1 collective-permute-done.11.refs_2_
  110.8 1.3 %put.7 = bf16[96,8,4096]{2,1,0:T(8,128)(2,1)} custom-call(s32[1]{0:T(128)} %bitcast.place, bf16[96,8,4096]{2,1,0:T(8,128)(2,1)} %put.6.refs_0_, bf16[12,8,4096]{2,1,0:T(8,128)(2,1)S(1)} %collective-permute-done.10.refs_1_, bf16[12,8,4096]{2,1,0:T(8,128)(2,1)S(1)} %collective-permute-done.11.refs_2_), custom_call_target="tpu_custom_call", output_to_operand_aliasing={{}: (1, {})} | custom-call | tf_op jit(solution)/shard_map/put/pallas_call | solution.py:166
  (17 shorter events, 0.1 us)
Async XLA Ops:
  0.6 0.9 copy-start
  1.5 0.9 copy-start.1
  2.4 0.9 copy-start.2
  3.3 0.9 copy-start.3
  49.8 10.2 %collective-permute-start = (bf16[1,8,4096]{2,1,0:T(8,128)(2,1)S(1)}, bf16[1,8,4096]{2,1,0:T(8,128)(2,1)S(1)}, u32[]{:S(2)}, u32[]{:S(2)}) collective-permute-start(bf16[1,8,4096]{2,1,0:T(8,128)(2,1)S(1)} %weights.1), channel_id=1, source_target_pairs={{0,32},{1,33},{2,34},{3,35},{4,36},{5,37},{6,38},{7,39},{8,72},{9,... | collective-permute-start | bytes 196616 | tf_op jit(solution)/shard_map/ppermute | solution.py:182
  52.6 10.5 %collective-permute-start.1 = (bf16[1,8,4096]{2,1,0:T(8,128)(2,1)S(1)}, bf16[1,8,4096]{2,1,0:T(8,128)(2,1)S(1)}, u32[]{:S(2)}, u32[]{:S(2)}) collective-permute-start(bf16[1,8,4096]{2,1,0:T(8,128)(2,1)S(1)} %weights.1), channel_id=1, source_target_pairs={{0,64},{1,65},{2,66},{3,67},{4,68},{5,69},{6,70},{7,71},{8,40},{9,... | collective-permute-start | bytes 196616 | tf_op jit(solution)/shard_map/ppermute | solution.py:182
  63.1 8.4 %collective-permute-start.2 = (bf16[3,8,4096]{2,1,0:T(8,128)(2,1)S(1)}, bf16[3,8,4096]{2,1,0:T(8,128)(2,1)S(1)}, u32[]{:S(2)}, u32[]{:S(2)}) collective-permute-start(bf16[3,8,4096]{2,1,0:T(8,128)(2,1)S(1)} %pad_maximum_fusion), channel_id=1, source_target_pairs={{0,2},{1,9},{2,0},{3,11},{4,6},{5,13},{6,4},{7,15},{8,10},{9,1},{1... | collective-permute-start | bytes 589832 | tf_op jit(solution)/shard_map/ppermute | solution.py:182
  65.9 7.6 %collective-permute-start.3 = (bf16[3,8,4096]{2,1,0:T(8,128)(2,1)S(1)}, bf16[3,8,4096]{2,1,0:T(8,128)(2,1)S(1)}, u32[]{:S(2)}, u32[]{:S(2)}) collective-permute-start(bf16[3,8,4096]{2,1,0:T(8,128)(2,1)S(1)} %pad_maximum_fusion), channel_id=1, source_target_pairs={{0,6},{1,89},{2,4},{3,91},{4,2},{5,93},{6,0},{7,95},{8,14},{9,17},... | collective-permute-start | bytes 589832 | tf_op jit(solution)/shard_map/ppermute | solution.py:182
  68.4 8.5 %collective-permute-start.4 = (bf16[3,8,4096]{2,1,0:T(8,128)(2,1)S(1)}, bf16[3,8,4096]{2,1,0:T(8,128)(2,1)S(1)}, u32[]{:S(2)}, u32[]{:S(2)}) collective-permute-start(bf16[3,8,4096]{2,1,0:T(8,128)(2,1)S(1)} %pad_maximum_fusion), channel_id=1, source_target_pairs={{0,4},{1,17},{2,6},{3,19},{4,0},{5,21},{6,2},{7,23},{8,12},{9,89},... | collective-permute-start | bytes 589832 | tf_op jit(solution)/shard_map/ppermute | solution.py:182
  76.9 14.3 %collective-permute-start.7 = (bf16[12,8,4096]{2,1,0:T(8,128)(2,1)S(1)}, bf16[12,8,4096]{2,1,0:T(8,128)(2,1)}, u32[]{:S(2)}, u32[]{:S(2)}) collective-permute-start(bf16[12,8,4096]{2,1,0:T(8,128)(2,1)S(1)} %constant_dynamic-update-slice_fusion.refs_0_), channel_id=1, source_target_pairs={{0,1},{1,0},{2,3},{3,2},{4,5},{5,4},{6,7},{7,6},{8,9},{9,8},{10,11... | collective-permute-start | bytes 2359304 | tf_op jit(solution)/shard_map/ppermute | solution.py:182
  82.2 14.6 %collective-permute-start.6 = (bf16[12,8,4096]{2,1,0:T(8,128)(2,1)S(1)}, bf16[12,8,4096]{2,1,0:T(8,128)(2,1)S(1)}, u32[]{:S(2)}, u32[]{:S(2)}) collective-permute-start(bf16[12,8,4096]{2,1,0:T(8,128)(2,1)S(1)} %constant_dynamic-update-slice_fusion.refs_0_), channel_id=1, source_target_pairs={{0,16},{1,5},{2,18},{3,7},{4,20},{5,1},{6,22},{7,3},{8,88},{9,13},... | collective-permute-start | bytes 2359304 | tf_op jit(solution)/shard_map/ppermute | solution.py:182
  86.2 18.4 %collective-permute-start.5 = (bf16[12,8,4096]{2,1,0:T(8,128)(2,1)S(1)}, bf16[12,8,4096]{2,1,0:T(8,128)(2,1)S(1)}, u32[]{:S(2)}, u32[]{:S(2)}) collective-permute-start(bf16[12,8,4096]{2,1,0:T(8,128)(2,1)S(1)} %constant_dynamic-update-slice_fusion.refs_0_), channel_id=1, source_target_pairs={{0,8},{1,3},{2,10},{3,1},{4,12},{5,7},{6,14},{7,5},{8,0},{9,11},{1... | collective-permute-start | bytes 2359304 | tf_op jit(solution)/shard_map/ppermute | solution.py:182
  88.4 18.1 %collective-permute-start.8 = (bf16[12,8,4096]{2,1,0:T(8,128)(2,1)S(1)}, bf16[12,8,4096]{2,1,0:T(8,128)(2,1)S(1)}, u32[]{:S(2)}, u32[]{:S(2)}) collective-permute-start(bf16[12,8,4096]{2,1,0:T(8,128)(2,1)S(1)} %constant_dynamic-update-slice_fusion.refs_0_), channel_id=1, source_target_pairs={{0,88},{1,7},{2,90},{3,5},{4,92},{5,3},{6,94},{7,1},{8,16},{9,15},... | collective-permute-start | bytes 2359304 | tf_op jit(solution)/shard_map/ppermute | solution.py:182
  96.8 12.1 %collective-permute-start.9 = (bf16[12,8,4096]{2,1,0:T(8,128)(2,1)S(1)}, bf16[12,8,4096]{2,1,0:T(8,128)(2,1)S(1)}, u32[]{:S(2)}, u32[]{:S(2)}) collective-permute-start(bf16[12,8,4096]{2,1,0:T(8,128)(2,1)S(1)} %collective-permute-done.6.refs_1_), channel_id=1, source_target_pairs={{0,1},{1,0},{2,3},{3,2},{4,5},{5,4},{6,7},{7,6},{8,9},{9,8},{10,11... | collective-permute-start | bytes 2359304 | tf_op jit(solution)/shard_map/ppermute | solution.py:182
  104.6 6.1 %collective-permute-start.10 = (bf16[12,8,4096]{2,1,0:T(8,128)(2,1)S(1)}, bf16[12,8,4096]{2,1,0:T(8,128)(2,1)S(1)}, u32[]{:S(2)}, u32[]{:S(2)}) collective-permute-start(bf16[12,8,4096]{2,1,0:T(8,128)(2,1)S(1)} %collective-permute-done.5.refs_1_), channel_id=1, source_target_pairs={{0,1},{1,0},{2,3},{3,2},{4,5},{5,4},{6,7},{7,6},{8,9},{9,8},{10,11... | collective-permute-start | bytes 2359304 | tf_op jit(solution)/shard_map/ppermute | solution.py:182
  106.5 4.3 %collective-permute-start.11 = (bf16[12,8,4096]{2,1,0:T(8,128)(2,1)S(1)}, bf16[12,8,4096]{2,1,0:T(8,128)(2,1)S(1)}, u32[]{:S(2)}, u32[]{:S(2)}) collective-permute-start(bf16[12,8,4096]{2,1,0:T(8,128)(2,1)S(1)} %collective-permute-done.8.refs_2_), channel_id=1, source_target_pairs={{0,1},{1,0},{2,3},{3,2},{4,5},{5,4},{6,7},{7,6},{8,9},{9,8},{10,11... | collective-permute-start | bytes 2359304 | tf_op jit(solution)/shard_map/ppermute | solution.py:182

commit v2 on v1

--- a/solution.py
+++ b/solution.py
@@ -47,7 +47,7 @@
         in_specs=[pl.BlockSpec(memory_space=pltpu.HBM)] * 4,
         out_specs=[pl.BlockSpec(memory_space=pltpu.VMEM)] * 5,
         scratch_shapes=[pltpu.SemaphoreType.DMA((4,))],
-        compiler_params=small(),
+        compiler_params=pltpu.CompilerParams(vmem_limit_bytes=54656 * 1024),
         name="spread_squares",
     )(*state)
 
@@ -191,10 +191,10 @@
     for s in (1, -1, 2):
         own.append(sent(two, near(s, 0)))
     other = {0: swap(own[0])}
-    out = put(place, None, [(own[0], 0, False), (other[0], 0, True)])
+    out = put(place, None, [(own[0], 0, False)])
     own[3], out = lax.optimization_barrier((own[3], out))
     other[3] = swap(own[3])
-    out = put(place, out, [(own[3], 3, False)])
+    out = put(place, out, [(own[3], 3, False), (other[0], 0, True)])
     own[1], out = lax.optimization_barrier((own[1], out))
     other[1] = swap(own[1])
     other[2] = swap(own[2])

time: 113 us -> 107 us (0.947)
  waiting for transfers between devices: 15 us -> 8.75 us
  starting transfers between devices: 39.6 us -> 43.5 us
  local copies, waits for them, and re-layouts: 3.67 us -> 0.06 us
    ppermute x12, waiting for transfers between devices: 15 us -> 8.75 us  [gathered(): sent = lambda x, target: lax.ppermute(x, FSDP, pairs(target))]
    ppermute x12, starting transfers between devices: 39.6 us -> 43.5 us  [gathered(): sent = lambda x, target: lax.ppermute(x, FSDP, pairs(target))]
    unnamed x13 -> x5, local copies, waits for them, and re-layouts: 3.66 us -> 0.05 us
  transfers between devices with their start and end apart: 12 -> 12, of which waited for: 6 -> 5; matrix products, arithmetic and copies ran while one was open for 0% -> 0% of each run, Pallas kernels for 5% -> 6%
where the time goes in v2:
time: 107 us
  blocking collectives  44.4 us (41%)
  starting transfers between devices  43.5 us (41%)
  Pallas kernels  8.95 us (8%)
  waiting for transfers between devices  8.75 us (8%)
    all_to_all x2, blocking collectives, swapped(): return lax.all_to_all(x, axis, 0, 0, tiled=True)  44.4 us
    ppermute x12, starting transfers between devices, gathered(): sent = lambda x, target: lax.ppermute(x, FSDP, pairs(target))  43.5 us
    ppermute x12, waiting for transfers between devices, gathered(): sent = lambda x, target: lax.ppermute(x, FSDP, pairs(target))  8.75 us
    pallas_call x4, Pallas kernels, put(): pl.pallas_call(body, out_shape=jax.ShapeDtypeStruct((NZ * NX * NC, *first...  6.5 us
  transfers between devices with their start and end apart: 12, of which 5 were waited for; matrix products, arithmetic and copies ran while one was open for 0% of the time, Pallas kernels for 6%

profile of v2, /device:TPU:1, one launch (start us, length us, event | category | flops | bytes accessed | tf_op | source)
XLA Modules:
  0.0 106.6 jit_solution(3634164199958304927)
XLA Ops:
  0.6 1.1 %spread_squares.1 = (f32[64,1,128]{2,1,0:T(1,128)S(1)}, f32[1,8,4096]{2,1,0:T(8,128)S(1)}, f32[1,8,4096]{2,1,0:T(8,128)S(1)}, f32[1,8,4096]{2,1,0:T(8,128)S(1)}, f32[1,8,4096]{2,1,0:T(8,128)S(1)}) custom-call(f32[1,8,4096]{2,1,0:T(8,128)} %refs_0_.1, f32[1,8,4096]{2,1,0:T(8,128)} %refs_1_.1, f32[1,8,4096]{2,1,0:T(8,128)} %refs_2_.1, f32[1,8,4096]{2,1,0:T(8,128)} %refs_3_.1), custom_call_target="tpu_custom_call" | custom-call | tf_op jit(solution)/shard_map/spread_squares/pallas_call | solution.py:43
  1.8 23.2 %all_to_all.10.s = f32[64,1,128]{2,1,0:T(1,128)S(1)} all-to-all(f32[64,1,128]{2,1,0:T(1,128)S(1)} %get-tuple-element.24), channel_id=1, replica_groups=mesh['section'=8,'fsdp_0'=12,'fsdp_1'=4,'fsdp_2'=2] {'section','fsdp_1',..., dimensions={0} | all-to-all | bytes 65536 | tf_op jit(solution)/shard_map/all_to_all | solution.py:27
  25.0 0.1 summed_and_spread.1
  25.1 21.2 %all_to_all.11.s = f32[12,1,128]{2,1,0:T(1,128)S(1)} all-to-all(f32[12,1,128]{2,1,0:T(1,128)S(1)} %summed_and_spread.1), channel_id=1, replica_groups=mesh['section'=8,'fsdp_0'=12,'fsdp_1'=4,'fsdp_2'=2] {'fsdp_0'}, dimensions={0} | all-to-all | bytes 12288 | tf_op jit(solution)/shard_map/all_to_all | solution.py:27
  46.3 0.3 weights.1
  46.6 2.8 %collective-permute-start = (bf16[1,8,4096]{2,1,0:T(8,128)(2,1)S(1)}, bf16[1,8,4096]{2,1,0:T(8,128)(2,1)S(1)}, u32[]{:S(2)}, u32[]{:S(2)}) collective-permute-start(bf16[1,8,4096]{2,1,0:T(8,128)(2,1)S(1)} %weights.1), channel_id=1, source_target_pairs={{0,32},{1,33},{2,34},{3,35},{4,36},{5,37},{6,38},{7,39},{8,72},{9,... | collective-permute-start | bytes 196616 | tf_op jit(solution)/shard_map/ppermute | solution.py:182
  49.4 6.4 %collective-permute-start.1 = (bf16[1,8,4096]{2,1,0:T(8,128)(2,1)S(1)}, bf16[1,8,4096]{2,1,0:T(8,128)(2,1)S(1)}, u32[]{:S(2)}, u32[]{:S(2)}) collective-permute-start(bf16[1,8,4096]{2,1,0:T(8,128)(2,1)S(1)} %weights.1), channel_id=1, source_target_pairs={{0,64},{1,65},{2,66},{3,67},{4,68},{5,69},{6,70},{7,71},{8,40},{9,... | collective-permute-start | bytes 196616 | tf_op jit(solution)/shard_map/ppermute | solution.py:182
  55.8 1.0 state.1
  56.8 0.0 collective-permute-done
  56.8 3.1 %collective-permute-done.1 = bf16[1,8,4096]{2,1,0:T(8,128)(2,1)S(1)} collective-permute-done((bf16[1,8,4096]{2,1,0:T(8,128)(2,1)S(1)}, bf16[1,8,4096]{2,1,0:T(8,128)(2,1)S(1)}, u32[]{:S(2)}, u32[]{:S(2)}) %collective-permute-start.1) | collective-permute-done | bytes 65568 | tf_op jit(solution)/shard_map/ppermute | solution.py:182
  59.9 2.8 %collective-permute-start.2 = (bf16[3,8,4096]{2,1,0:T(8,128)(2,1)S(1)}, bf16[3,8,4096]{2,1,0:T(8,128)(2,1)S(1)}, u32[]{:S(2)}, u32[]{:S(2)}) collective-permute-start(bf16[3,8,4096]{2,1,0:T(8,128)(2,1)S(1)} %pad_maximum_fusion), channel_id=1, source_target_pairs={{0,2},{1,9},{2,0},{3,11},{4,6},{5,13},{6,4},{7,15},{8,10},{9,1},{1... | collective-permute-start | bytes 589832 | tf_op jit(solution)/shard_map/ppermute | solution.py:182
  62.7 2.5 %collective-permute-start.3 = (bf16[3,8,4096]{2,1,0:T(8,128)(2,1)S(1)}, bf16[3,8,4096]{2,1,0:T(8,128)(2,1)S(1)}, u32[]{:S(2)}, u32[]{:S(2)}) collective-permute-start(bf16[3,8,4096]{2,1,0:T(8,128)(2,1)S(1)} %pad_maximum_fusion), channel_id=1, source_target_pairs={{0,6},{1,89},{2,4},{3,91},{4,2},{5,93},{6,0},{7,95},{8,14},{9,17},... | collective-permute-start | bytes 589832 | tf_op jit(solution)/shard_map/ppermute | solution.py:182
  65.2 3.1 %collective-permute-start.4 = (bf16[3,8,4096]{2,1,0:T(8,128)(2,1)S(1)}, bf16[3,8,4096]{2,1,0:T(8,128)(2,1)S(1)}, u32[]{:S(2)}, u32[]{:S(2)}) collective-permute-start(bf16[3,8,4096]{2,1,0:T(8,128)(2,1)S(1)} %pad_maximum_fusion), channel_id=1, source_target_pairs={{0,4},{1,17},{2,6},{3,19},{4,0},{5,21},{6,2},{7,23},{8,12},{9,89},... | collective-permute-start | bytes 589832 | tf_op jit(solution)/shard_map/ppermute | solution.py:182
  68.3 0.0 collective-permute-done.2
  68.3 1.9 %collective-permute-done.3 = bf16[3,8,4096]{2,1,0:T(8,128)(2,1)S(1)} collective-permute-done((bf16[3,8,4096]{2,1,0:T(8,128)(2,1)S(1)}, bf16[3,8,4096]{2,1,0:T(8,128)(2,1)S(1)}, u32[]{:S(2)}, u32[]{:S(2)}) %collective-permute-start.3) | collective-permute-done | bytes 196640 | tf_op jit(solution)/shard_map/ppermute | solution.py:182
  70.3 3.4 %collective-permute-done.4 = bf16[3,8,4096]{2,1,0:T(8,128)(2,1)S(1)} collective-permute-done((bf16[3,8,4096]{2,1,0:T(8,128)(2,1)S(1)}, bf16[3,8,4096]{2,1,0:T(8,128)(2,1)S(1)}, u32[]{:S(2)}, u32[]{:S(2)}) %collective-permute-start.4) | collective-permute-done | bytes 196640 | tf_op jit(solution)/shard_map/ppermute | solution.py:182
  73.7 2.9 %collective-permute-start.6 = (bf16[12,8,4096]{2,1,0:T(8,128)(2,1)S(1)}, bf16[12,8,4096]{2,1,0:T(8,128)(2,1)S(1)}, u32[]{:S(2)}, u32[]{:S(2)}) collective-permute-start(bf16[12,8,4096]{2,1,0:T(8,128)(2,1)S(1)} %constant_dynamic-update-slice_fusion.refs_0_), channel_id=1, source_target_pairs={{0,16},{1,5},{2,18},{3,7},{4,20},{5,1},{6,22},{7,3},{8,88},{9,13},... | collective-permute-start | bytes 2359304 | tf_op jit(solution)/shard_map/ppermute | solution.py:182
  76.6 4.3 %collective-permute-start.7 = (bf16[12,8,4096]{2,1,0:T(8,128)(2,1)S(1)}, bf16[12,8,4096]{2,1,0:T(8,128)(2,1)}, u32[]{:S(2)}, u32[]{:S(2)}) collective-permute-start(bf16[12,8,4096]{2,1,0:T(8,128)(2,1)S(1)} %constant_dynamic-update-slice_fusion.refs_0_), channel_id=1, source_target_pairs={{0,1},{1,0},{2,3},{3,2},{4,5},{5,4},{6,7},{7,6},{8,9},{9,8},{10,11... | collective-permute-start | bytes 2359304 | tf_op jit(solution)/shard_map/ppermute | solution.py:182
  80.9 2.3 %collective-permute-start.5 = (bf16[12,8,4096]{2,1,0:T(8,128)(2,1)S(1)}, bf16[12,8,4096]{2,1,0:T(8,128)(2,1)S(1)}, u32[]{:S(2)}, u32[]{:S(2)}) collective-permute-start(bf16[12,8,4096]{2,1,0:T(8,128)(2,1)S(1)} %constant_dynamic-update-slice_fusion.refs_0_), channel_id=1, source_target_pairs={{0,8},{1,3},{2,10},{3,1},{4,12},{5,7},{6,14},{7,5},{8,0},{9,11},{1... | collective-permute-start | bytes 2359304 | tf_op jit(solution)/shard_map/ppermute | solution.py:182
  83.3 3.8 %collective-permute-start.8 = (bf16[12,8,4096]{2,1,0:T(8,128)(2,1)S(1)}, bf16[12,8,4096]{2,1,0:T(8,128)(2,1)S(1)}, u32[]{:S(2)}, u32[]{:S(2)}) collective-permute-start(bf16[12,8,4096]{2,1,0:T(8,128)(2,1)S(1)} %constant_dynamic-update-slice_fusion.refs_0_), channel_id=1, source_target_pairs={{0,88},{1,7},{2,90},{3,5},{4,92},{5,3},{6,94},{7,1},{8,16},{9,15},... | collective-permute-start | bytes 2359304 | tf_op jit(solution)/shard_map/ppermute | solution.py:182
  87.1 1.0 put.4.refs_0_
  88.1 0.2 collective-permute-done.6.refs_1_
  88.2 6.8 %collective-permute-start.9 = (bf16[12,8,4096]{2,1,0:T(8,128)(2,1)S(1)}, bf16[12,8,4096]{2,1,0:T(8,128)(2,1)S(1)}, u32[]{:S(2)}, u32[]{:S(2)}) collective-permute-start(bf16[12,8,4096]{2,1,0:T(8,128)(2,1)S(1)} %collective-permute-done.6.refs_1_), channel_id=1, source_target_pairs={{0,1},{1,0},{2,3},{3,2},{4,5},{5,4},{6,7},{7,6},{8,9},{9,8},{10,11... | collective-permute-start | bytes 2359304 | tf_op jit(solution)/shard_map/ppermute | solution.py:182
  95.1 2.5 %put.5.refs_0_ = bf16[96,8,4096]{2,1,0:T(8,128)(2,1)} custom-call(s32[1]{0:T(128)} %bitcast.place, bf16[96,8,4096]{2,1,0:T(8,128)(2,1)} %put.4.refs_0_, bf16[12,8,4096]{2,1,0:T(8,128)(2,1)S(1)} %collective-permute-done.6.refs_1_, bf16[12,8,4096]{2,1,0:T(8,128)(2,1)} %collective-permute-done.7.refs_2_), custom_call_target="tpu_custom_call", output_to_operand_aliasing={{}: (1, {})} | custom-call | tf_op jit(solution)/shard_map/put/pallas_call | solution.py:166
  97.6 3.2 %collective-permute-start.10 = (bf16[12,8,4096]{2,1,0:T(8,128)(2,1)S(1)}, bf16[12,8,4096]{2,1,0:T(8,128)(2,1)S(1)}, u32[]{:S(2)}, u32[]{:S(2)}) collective-permute-start(bf16[12,8,4096]{2,1,0:T(8,128)(2,1)S(1)} %collective-permute-done.5.refs_1_), channel_id=1, source_target_pairs={{0,1},{1,0},{2,3},{3,2},{4,5},{5,4},{6,7},{7,6},{8,9},{9,8},{10,11... | collective-permute-start | bytes 2359304 | tf_op jit(solution)/shard_map/ppermute | solution.py:182
  100.8 0.0 collective-permute-done.8.refs_2_
  100.8 2.6 %collective-permute-start.11 = (bf16[12,8,4096]{2,1,0:T(8,128)(2,1)S(1)}, bf16[12,8,4096]{2,1,0:T(8,128)(2,1)S(1)}, u32[]{:S(2)}, u32[]{:S(2)}) collective-permute-start(bf16[12,8,4096]{2,1,0:T(8,128)(2,1)S(1)} %collective-permute-done.8.refs_2_), channel_id=1, source_target_pairs={{0,1},{1,0},{2,3},{3,2},{4,5},{5,4},{6,7},{7,6},{8,9},{9,8},{10,11... | collective-permute-start | bytes 2359304 | tf_op jit(solution)/shard_map/ppermute | solution.py:182
  103.4 0.0 collective-permute-done.9.refs_3_
  103.4 1.7 %put.6.refs_0_ = bf16[96,8,4096]{2,1,0:T(8,128)(2,1)} custom-call(s32[1]{0:T(128)} %bitcast.place, bf16[96,8,4096]{2,1,0:T(8,128)(2,1)} %put.5.refs_0_, bf16[12,8,4096]{2,1,0:T(8,128)(2,1)S(1)} %collective-permute-done.5.refs_1_, bf16[12,8,4096]{2,1,0:T(8,128)(2,1)S(1)} %collective-permute-done.8.refs_2_, ...), custom_call_target="tpu_custom_call", output_to_operand_aliasing={{}: (1, {})} | custom-call | tf_op jit(solution)/shard_map/put/pallas_call | solution.py:166
  105.2 0.0 collective-permute-done.10.refs_1_
  105.2 0.1 collective-permute-done.11.refs_2_
  105.3 1.3 %put.7 = bf16[96,8,4096]{2,1,0:T(8,128)(2,1)} custom-call(s32[1]{0:T(128)} %bitcast.place, bf16[96,8,4096]{2,1,0:T(8,128)(2,1)} %put.6.refs_0_, bf16[12,8,4096]{2,1,0:T(8,128)(2,1)S(1)} %collective-permute-done.10.refs_1_, bf16[12,8,4096]{2,1,0:T(8,128)(2,1)S(1)} %collective-permute-done.11.refs_2_), custom_call_target="tpu_custom_call", output_to_operand_aliasing={{}: (1, {})} | custom-call | tf_op jit(solution)/shard_map/put/pallas_call | solution.py:166
  (9 shorter events, 0.1 us)
Async XLA Ops:
  46.6 10.2 %collective-permute-start = (bf16[1,8,4096]{2,1,0:T(8,128)(2,1)S(1)}, bf16[1,8,4096]{2,1,0:T(8,128)(2,1)S(1)}, u32[]{:S(2)}, u32[]{:S(2)}) collective-permute-start(bf16[1,8,4096]{2,1,0:T(8,128)(2,1)S(1)} %weights.1), channel_id=1, source_target_pairs={{0,32},{1,33},{2,34},{3,35},{4,36},{5,37},{6,38},{7,39},{8,72},{9,... | collective-permute-start | bytes 196616 | tf_op jit(solution)/shard_map/ppermute | solution.py:182
  49.4 10.5 %collective-permute-start.1 = (bf16[1,8,4096]{2,1,0:T(8,128)(2,1)S(1)}, bf16[1,8,4096]{2,1,0:T(8,128)(2,1)S(1)}, u32[]{:S(2)}, u32[]{:S(2)}) collective-permute-start(bf16[1,8,4096]{2,1,0:T(8,128)(2,1)S(1)} %weights.1), channel_id=1, source_target_pairs={{0,64},{1,65},{2,66},{3,67},{4,68},{5,69},{6,70},{7,71},{8,40},{9,... | collective-permute-start | bytes 196616 | tf_op jit(solution)/shard_map/ppermute | solution.py:182
  59.9 8.4 %collective-permute-start.2 = (bf16[3,8,4096]{2,1,0:T(8,128)(2,1)S(1)}, bf16[3,8,4096]{2,1,0:T(8,128)(2,1)S(1)}, u32[]{:S(2)}, u32[]{:S(2)}) collective-permute-start(bf16[3,8,4096]{2,1,0:T(8,128)(2,1)S(1)} %pad_maximum_fusion), channel_id=1, source_target_pairs={{0,2},{1,9},{2,0},{3,11},{4,6},{5,13},{6,4},{7,15},{8,10},{9,1},{1... | collective-permute-start | bytes 589832 | tf_op jit(solution)/shard_map/ppermute | solution.py:182
  62.7 7.6 %collective-permute-start.3 = (bf16[3,8,4096]{2,1,0:T(8,128)(2,1)S(1)}, bf16[3,8,4096]{2,1,0:T(8,128)(2,1)S(1)}, u32[]{:S(2)}, u32[]{:S(2)}) collective-permute-start(bf16[3,8,4096]{2,1,0:T(8,128)(2,1)S(1)} %pad_maximum_fusion), channel_id=1, source_target_pairs={{0,6},{1,89},{2,4},{3,91},{4,2},{5,93},{6,0},{7,95},{8,14},{9,17},... | collective-permute-start | bytes 589832 | tf_op jit(solution)/shard_map/ppermute | solution.py:182
  65.2 8.5 %collective-permute-start.4 = (bf16[3,8,4096]{2,1,0:T(8,128)(2,1)S(1)}, bf16[3,8,4096]{2,1,0:T(8,128)(2,1)S(1)}, u32[]{:S(2)}, u32[]{:S(2)}) collective-permute-start(bf16[3,8,4096]{2,1,0:T(8,128)(2,1)S(1)} %pad_maximum_fusion), channel_id=1, source_target_pairs={{0,4},{1,17},{2,6},{3,19},{4,0},{5,21},{6,2},{7,23},{8,12},{9,89},... | collective-permute-start | bytes 589832 | tf_op jit(solution)/shard_map/ppermute | solution.py:182
  73.7 14.5 %collective-permute-start.6 = (bf16[12,8,4096]{2,1,0:T(8,128)(2,1)S(1)}, bf16[12,8,4096]{2,1,0:T(8,128)(2,1)S(1)}, u32[]{:S(2)}, u32[]{:S(2)}) collective-permute-start(bf16[12,8,4096]{2,1,0:T(8,128)(2,1)S(1)} %constant_dynamic-update-slice_fusion.refs_0_), channel_id=1, source_target_pairs={{0,16},{1,5},{2,18},{3,7},{4,20},{5,1},{6,22},{7,3},{8,88},{9,13},... | collective-permute-start | bytes 2359304 | tf_op jit(solution)/shard_map/ppermute | solution.py:182
  76.6 18.5 %collective-permute-start.7 = (bf16[12,8,4096]{2,1,0:T(8,128)(2,1)S(1)}, bf16[12,8,4096]{2,1,0:T(8,128)(2,1)}, u32[]{:S(2)}, u32[]{:S(2)}) collective-permute-start(bf16[12,8,4096]{2,1,0:T(8,128)(2,1)S(1)} %constant_dynamic-update-slice_fusion.refs_0_), channel_id=1, source_target_pairs={{0,1},{1,0},{2,3},{3,2},{4,5},{5,4},{6,7},{7,6},{8,9},{9,8},{10,11... | collective-permute-start | bytes 2359304 | tf_op jit(solution)/shard_map/ppermute | solution.py:182
  80.9 16.6 %collective-permute-start.5 = (bf16[12,8,4096]{2,1,0:T(8,128)(2,1)S(1)}, bf16[12,8,4096]{2,1,0:T(8,128)(2,1)S(1)}, u32[]{:S(2)}, u32[]{:S(2)}) collective-permute-start(bf16[12,8,4096]{2,1,0:T(8,128)(2,1)S(1)} %constant_dynamic-update-slice_fusion.refs_0_), channel_id=1, source_target_pairs={{0,8},{1,3},{2,10},{3,1},{4,12},{5,7},{6,14},{7,5},{8,0},{9,11},{1... | collective-permute-start | bytes 2359304 | tf_op jit(solution)/shard_map/ppermute | solution.py:182
  83.3 17.5 %collective-permute-start.8 = (bf16[12,8,4096]{2,1,0:T(8,128)(2,1)S(1)}, bf16[12,8,4096]{2,1,0:T(8,128)(2,1)S(1)}, u32[]{:S(2)}, u32[]{:S(2)}) collective-permute-start(bf16[12,8,4096]{2,1,0:T(8,128)(2,1)S(1)} %constant_dynamic-update-slice_fusion.refs_0_), channel_id=1, source_target_pairs={{0,88},{1,7},{2,90},{3,5},{4,92},{5,3},{6,94},{7,1},{8,16},{9,15},... | collective-permute-start | bytes 2359304 | tf_op jit(solution)/shard_map/ppermute | solution.py:182
  88.2 15.2 %collective-permute-start.9 = (bf16[12,8,4096]{2,1,0:T(8,128)(2,1)S(1)}, bf16[12,8,4096]{2,1,0:T(8,128)(2,1)S(1)}, u32[]{:S(2)}, u32[]{:S(2)}) collective-permute-start(bf16[12,8,4096]{2,1,0:T(8,128)(2,1)S(1)} %collective-permute-done.6.refs_1_), channel_id=1, source_target_pairs={{0,1},{1,0},{2,3},{3,2},{4,5},{5,4},{6,7},{7,6},{8,9},{9,8},{10,11... | collective-permute-start | bytes 2359304 | tf_op jit(solution)/shard_map/ppermute | solution.py:182
  97.6 7.6 %collective-permute-start.10 = (bf16[12,8,4096]{2,1,0:T(8,128)(2,1)S(1)}, bf16[12,8,4096]{2,1,0:T(8,128)(2,1)S(1)}, u32[]{:S(2)}, u32[]{:S(2)}) collective-permute-start(bf16[12,8,4096]{2,1,0:T(8,128)(2,1)S(1)} %collective-permute-done.5.refs_1_), channel_id=1, source_target_pairs={{0,1},{1,0},{2,3},{3,2},{4,5},{5,4},{6,7},{7,6},{8,9},{9,8},{10,11... | collective-permute-start | bytes 2359304 | tf_op jit(solution)/shard_map/ppermute | solution.py:182
  100.8 4.5 %collective-permute-start.11 = (bf16[12,8,4096]{2,1,0:T(8,128)(2,1)S(1)}, bf16[12,8,4096]{2,1,0:T(8,128)(2,1)S(1)}, u32[]{:S(2)}, u32[]{:S(2)}) collective-permute-start(bf16[12,8,4096]{2,1,0:T(8,128)(2,1)S(1)} %collective-permute-done.8.refs_2_), channel_id=1, source_target_pairs={{0,1},{1,0},{2,3},{3,2},{4,5},{5,4},{6,7},{7,6},{8,9},{9,8},{10,11... | collective-permute-start | bytes 2359304 | tf_op jit(solution)/shard_map/ppermute | solution.py:182
